TPU v7x, 32 devices: a whole 2x2x4 slice. The times are simulated.
32 devices in a mesh: gx: 4 (over z), gy: 4 (over y, x), gz: 2 (over core).
Axes of the slice: x: 2, y: 2, z: 4, core: 2. Of those that a mesh axis runs over, the one named last changes fastest.
Arguments:
- signal: float32 [16, 131072], P(None, ('gx', 'gy', 'gz')), may hold values from -6 to 6
- order: int32 [131072], P(('gx', 'gy', 'gz')), may hold values from 0 to 4095, as said below
- near_tiles: bfloat16 [512, 3, 256, 256], P(('gx', 'gy', 'gz')), may hold values from -0.21875 to 0.21875
- near_list: int32 [512, 3], P(('gx', 'gy', 'gz')), may hold values from 0 to 511, as said below
- leaf_basis: bfloat16 [512, 64, 256], P(('gx', 'gy', 'gz')), may hold values from -0.375 to 0.375
- leaf_transfer: bfloat16 [512, 64, 64], P(('gx', 'gy', 'gz')), may hold values from -0.5 to 0.5
- leaf_coupling: bfloat16 [512, 64, 192], P(('gx', 'gy', 'gz')), may hold values from -0.4375 to 0.4375
- leaf_links: int32 [512, 3], P(('gx', 'gy', 'gz')), may hold values from 0 to 511, as said below
- device_transfer: bfloat16 [32, 64, 64], P(('gx', 'gy', 'gz')), may hold values from -0.5 to 0.5
- device_coupling: bfloat16 [32, 64, 192], P(('gx', 'gy', 'gz')), may hold values from -0.15625 to 0.15625
- device_links: int32 [32, 3], P(('gx', 'gy', 'gz')), may hold values from 0 to 31, as said below
- block_transfer: bfloat16 [16, 64, 64], P(('gx', 'gy')), may hold values from -0.5 to 0.5
- block_coupling: bfloat16 [16, 64, 192], P(('gx', 'gy')), may hold values from -0.15625 to 0.15625
- block_links: int32 [16, 3], P(('gx', 'gy')), may hold values from 0 to 15, as said below
- top_coupling: bfloat16 [4, 64, 192], P('gx'), may hold values from -0.109375 to 0.109375
- top_links: int32 [4, 3], P('gx'), may hold values from 0 to 3, as said below
Outputs:
- smoothed: float32 [16, 131072], P(None, ('gx', 'gy', 'gz'))
- twice: float32 [16, 131072], P(None, ('gx', 'gy', 'gz'))
Inputs may be any that keep to these rules, and one draw needn't show every extreme that they name: `order`: each device's block of 4096 consecutive entries is a permutation of 0 to 4095. `near_list`: row i holds i first, then two different leaves j with 1 <= |j - i| <= 2. `leaf_links`: row i holds three different leaves j with 2 <= |j - i| <= 4. `device_links`: row i holds three different device clusters j with 1 <= |j - i| <= 3. `block_links`: row i holds three different second-level clusters other than i. `top_links`: row i holds three different first-level clusters other than i.
All inputs are finite; a program needn't handle non-finite values.
Results may differ from a plain program's by a relative error of at most 0.0043.
Values may be sent and summed in bfloat16 or wider, within the bound.
No kernel may reach another device: no remote copies, remote signals or barrier semaphores. Data moves between devices by JAX's collectives and lax.ppermute only.
A program may use at most 64 MiB of HBM per device.

v0:
```python
import jax
import jax.numpy as jnp
from jax import lax
from jax.sharding import PartitionSpec as P

NEAR_REACH = 2
LINK_REACH = 4
DEVICE_REACH = 3
HIGH = lax.Precision.HIGHEST


def shifted(block, axis, distance):
    devices = range(lax.axis_size(axis))
    route = [(i - distance, i) for i in devices if i - distance in devices]
    return lax.ppermute(block, axis, route)


def couple(picked, coupling):
    rank_dim = coupling.shape[0]
    link_count = picked.shape[0]
    table = coupling.astype(jnp.float32).reshape(rank_dim, link_count, rank_dim)
    return jnp.einsum("jrk,kjm->rm", picked, table, precision=HIGH)


def spread_down(parent, transfer):
    return jnp.dot(parent, transfer.astype(jnp.float32).T, precision=HIGH)


def relay_side(own_moment, direction):
    window = own_moment[None][:0]
    for step in range(DEVICE_REACH):
        outgoing = jnp.concatenate([own_moment[None], window], axis=0)
        window = shifted(outgoing, ("gx", "gy", "gz"), direction)
    return window


def apply_matrix(
    leaves,
    near_tiles,
    near_list,
    leaf_basis,
    leaf_transfer,
    leaf_coupling,
    leaf_links,
    device_transfer,
    device_coupling,
    device_links,
    block_transfer,
    block_coupling,
    block_links,
    top_coupling,
    top_links,
):
    leaf_dev = leaves.shape[1]
    device = lax.axis_index(("gx", "gy", "gz"))
    first_leaf = device * leaf_dev
    rims = []
    for offset, edge in ((1, leaves[:, leaf_dev - NEAR_REACH :]), (-1, leaves[:, :NEAR_REACH])):
        rims.append(shifted(edge, ("gx", "gy", "gz"), offset))
    widened = jnp.concatenate([rims[0], leaves, rims[1]], axis=1)
    moments = jnp.einsum("rls,lks->rlk", leaves, leaf_basis, preferred_element_type=jnp.float32)
    edges = []
    for offset, edge in ((1, moments[:, leaf_dev - LINK_REACH :]), (-1, moments[:, :LINK_REACH])):
        edges.append(shifted(edge, ("gx", "gy", "gz"), offset))
    wide_moments = jnp.concatenate([edges[0], moments, edges[1]], axis=1)
    transfer_f = leaf_transfer.astype(jnp.float32)
    own_moment = jnp.einsum("rlk,lkm->rm", moments, transfer_f, precision=HIGH)
    block_term = jnp.dot(own_moment, device_transfer[0].astype(jnp.float32), precision=HIGH)
    block_moment = lax.psum(block_term, "gz")
    lower = relay_side(own_moment, 1)
    upper = relay_side(own_moment, -1)
    stacked = jnp.concatenate([lower[::-1], upper], axis=0)
    relative = device_links[0] - device
    position = relative + DEVICE_REACH - (relative > 0).astype(jnp.int32)
    device_picked = stacked[position]
    top_term = jnp.dot(block_moment, block_transfer[0].astype(jnp.float32), precision=HIGH)
    top_moment = lax.psum(top_term, "gy")
    every_top = lax.all_gather(top_moment[None], "gx", axis=0, tiled=True)
    every_block = lax.all_gather(block_moment[None], ("gx", "gy"), axis=0, tiled=True)
    top_field = couple(every_top[top_links[0]], top_coupling[0])
    block_field = couple(every_block[block_links[0]], block_coupling[0]) + spread_down(
        top_field, block_transfer[0]
    )
    device_field = couple(device_picked, device_coupling[0]) + spread_down(
        block_field, device_transfer[0]
    )
    local_links = leaf_links - first_leaf + LINK_REACH
    picked = wide_moments[:, local_links]
    rank_dim = leaf_coupling.shape[1]
    leaf_table = leaf_coupling.astype(jnp.float32).reshape(leaf_dev, rank_dim, -1, rank_dim)
    leaf_field = jnp.einsum("rljk,lkjm->rlm", picked, leaf_table, precision=HIGH)
    leaf_field = leaf_field + jnp.einsum("rm,lkm->rlk", device_field, transfer_f, precision=HIGH)
    far_part = jnp.einsum(
        "rlk,lks->rls",
        leaf_field.astype(jnp.bfloat16),
        leaf_basis,
        preferred_element_type=jnp.float32,
    )
    near_index = near_list - first_leaf + NEAR_REACH
    near_rows = widened[:, near_index]
    near_part = jnp.einsum(
        "rlns,lnst->rlt", near_rows, near_tiles, preferred_element_type=jnp.float32
    )
    return near_part + far_part


def shards(
    signal,
    order,
    near_tiles,
    near_list,
    leaf_basis,
    leaf_transfer,
    leaf_coupling,
    leaf_links,
    device_transfer,
    device_coupling,
    device_links,
    block_transfer,
    block_coupling,
    block_links,
    top_coupling,
    top_links,
):
    matrices = (
        near_tiles,
        near_list,
        leaf_basis,
        leaf_transfer,
        leaf_coupling,
        leaf_links,
        device_transfer,
        device_coupling,
        device_links,
        block_transfer,
        block_coupling,
        block_links,
        top_coupling,
        top_links,
    )
    rhs_count = signal.shape[0]
    leaf_count = near_tiles.shape[0]
    tree = jnp.take(signal, order, axis=1).astype(jnp.bfloat16).reshape(rhs_count, leaf_count, -1)
    first = apply_matrix(tree, *matrices)
    second = apply_matrix(first.astype(jnp.bfloat16), *matrices)
    empty = jnp.zeros_like(signal)
    smoothed = empty.at[:, order].set(first.reshape(rhs_count, -1))
    twice = empty.at[:, order].set(second.reshape(rhs_count, -1))
    return (smoothed, twice)


def solution(mesh):
    in_specs = (
        P(None, ("gx", "gy", "gz")),
        P(("gx", "gy", "gz")),
        P(("gx", "gy", "gz"), None, None, None),
        P(("gx", "gy", "gz"), None),
        P(("gx", "gy", "gz"), None, None),
        P(("gx", "gy", "gz"), None, None),
        P(("gx", "gy", "gz"), None, None),
        P(("gx", "gy", "gz"), None),
        P(("gx", "gy", "gz"), None, None),
        P(("gx", "gy", "gz"), None, None),
        P(("gx", "gy", "gz"), None),
        P(("gx", "gy"), None, None),
        P(("gx", "gy"), None, None),
        P(("gx", "gy"), None),
        P("gx", None, None),
        P("gx", None),
    )
    out_specs = (P(None, ("gx", "gy", "gz")), P(None, ("gx", "gy", "gz")))
    return jax.shard_map(shards, mesh=mesh, in_specs=in_specs, out_specs=out_specs, check_vma=False)
```

profile of v0, /device:TPU:4, one launch (start us, length us, event | category | flops | bytes accessed | tf_op | source)
XLA Modules:
  0.0 253.0 jit_solution(4829175544819906488)
XLA Ops:
  0.6 0.8 compare_and_fusion
  1.4 1.3 broadcast_clamp_fusion
  2.8 1.5 copy.38
  4.4 12.1 %gather_fusion = bf16[4096,16]{1,0:T(8,128)(2,1)S(1)} fusion(bf16[16,4096]{0,1:T(8,128)(2,1)S(1)} %copy.38, s32[4096]{0:T(1024)S(1)} %get-tuple-element.16), kind=kCustom, calls=%fused_computation | custom fusion | bytes 278528 | tf_op jit(solution)/shard_map/jit(_take)/gather | solution.py:143
  17.4 2.8 %collective-permute-start.7 = (f32[1,16,64]{2,1,0:T(8,128)S(1)}, f32[1,16,64]{2,1,0:T(8,128)S(1)}, u32[]{:S(2)}, u32[]{:S(2)}) collective-permute-start(f32[1,16,64]{2,1,0:T(8,128)S(1)} %bitcast.193), channel_id=1, source_target_pairs={{1,0},{2,1},{3,2},{4,3},{5,4},{6,5},{7,6},{8,7},{9,8},{10,9},{11,1... | collective-permute-start | bytes 12296 | tf_op jit(solution)/shard_map/ppermute | solution.py:15
  20.2 1.9 collective-permute-start.4
  22.2 2.6 %collective-permute-start = (bf16[16,2,256]{2,0,1:T(8,128)(2,1)S(1)}, bf16[16,2,256]{2,0,1:T(8,128)(2,1)S(1)}, u32[]{:S(2)}, u32[]{:S(2)}) collective-permute-start(bf16[16,2,256]{2,0,1:T(8,128)(2,1)S(1)} %get-tuple-element.14), channel_id=1, source_target_pairs={{0,1},{1,2},{2,3},{3,4},{4,5},{5,6},{6,7},{7,8},{8,9},{9,10},{10,1... | collective-permute-start | bytes 49160 | tf_op jit(solution)/shard_map/ppermute | solution.py:15
  24.8 3.8 %collective-permute-start.1 = (bf16[16,2,256]{2,0,1:T(8,128)(2,1)S(1)}, bf16[16,2,256]{2,0,1:T(8,128)(2,1)S(1)}, u32[]{:S(2)}, u32[]{:S(2)}) collective-permute-start(bf16[16,2,256]{2,0,1:T(8,128)(2,1)S(1)} %get-tuple-element.15), channel_id=1, source_target_pairs={{1,0},{2,1},{3,2},{4,3},{5,4},{6,5},{7,6},{8,7},{9,8},{10,9},{11,1... | collective-permute-start | bytes 49160 | tf_op jit(solution)/shard_map/ppermute | solution.py:15
  28.6 1.9 collective-permute-start.2
  31.3 3.6 %psum.28 = f32[16,64]{1,0:T(8,128)S(1)} all-reduce(f32[16,64]{1,0:T(8,128)S(1)} %fusion.23), channel_id=1, replica_groups=mesh['gx'=4,'gy'=4,'gz'=2] {'gz'}, use_global_device_ids=true, to_apply=%region_0.1 | all-reduce | flops 1024 | bytes 8192 | tf_op jit(solution)/shard_map/psum | solution.py:69
  34.9 35.5 %all-gather = f32[256,64]{1,0:T(8,128)S(1)} all-gather(f32[16,64]{1,0:T(8,128)S(1)} %psum.28), channel_id=2, replica_groups=mesh['gx'=4,'gy'=4,'gz'=2] {'gx','gy'}, dimensions={0}, use_global_device_ids=true | all-gather | bytes 69632 | tf_op jit(solution)/shard_map/all_gather | solution.py:79
  70.6 10.2 %psum.29 = f32[1,16,64]{2,1,0:T(8,128)S(1)} all-reduce(f32[1,16,64]{2,1,0:T(8,128)S(1)} %convolution_bitcast_fusion.11), channel_id=1, replica_groups=mesh['gx'=4,'gy'=4,'gz'=2] {'gy'}, use_global_device_ids=true, to_apply=%region_1.2 | all-reduce | flops 1024 | bytes 8192 | tf_op jit(solution)/shard_map/psum | solution.py:77
  80.8 13.1 %all_gather.13 = f32[4,16,64]{2,1,0:T(8,128)S(1)} all-gather(f32[1,16,64]{2,1,0:T(8,128)S(1)} %psum.29), channel_id=1, replica_groups=mesh['gx'=4,'gy'=4,'gz'=2] {'gx'}, dimensions={0}, use_global_device_ids=true | all-gather | bytes 20480 | tf_op jit(solution)/shard_map/all_gather | solution.py:78
  95.9 1.9 collective-permute-start.5
  97.8 4.5 %collective-permute-start.8 = (f32[2,16,64]{2,1,0:T(8,128)S(1)}, f32[2,16,64]{2,1,0:T(8,128)S(1)}, u32[]{:S(2)}, u32[]{:S(2)}) collective-permute-start(f32[2,16,64]{2,1,0:T(8,128)S(1)} %get-tuple-element.25), channel_id=1, source_target_pairs={{1,0},{2,1},{3,2},{4,3},{5,4},{6,5},{7,6},{8,7},{9,8},{10,9},{11,1... | collective-permute-start | bytes 24584 | tf_op jit(solution)/shard_map/ppermute | solution.py:15
  103.0 2.3 collective-permute-start.3
  105.3 2.0 collective-permute-start.6
  107.3 4.4 %collective-permute-start.9 = (f32[3,16,64]{2,1,0:T(8,128)S(1)}, f32[3,16,64]{2,1,0:T(8,128)S(1)}, u32[]{:S(2)}, u32[]{:S(2)}) collective-permute-start(f32[3,16,64]{2,1,0:T(8,128)S(1)} %get-tuple-element.23), channel_id=1, source_target_pairs={{1,0},{2,1},{3,2},{4,3},{5,4},{6,5},{7,6},{8,7},{9,8},{10,9},{11,1... | collective-permute-start | bytes 36872 | tf_op jit(solution)/shard_map/ppermute | solution.py:15
  112.4 3.7 %convolution_bitcast_fusion.1 = f32[16,16,256]{2,1,0:T(8,128)S(1)} fusion(bf16[16,16,3,256]{3,0,2,1:T(8,128)(2,1)S(1)} %bitcast.178, bf16[16,3,256,256]{3,2,1,0:T(8,128)(2,1)} %param.18), kind=kOutput, calls=%fused_computation.17 | convolution fusion | flops 100663296 | bytes 6946816 | tf_op jit(solution)/shard_map/rlns,lnst->rlt/dot_general | solution.py:101
  117.6 0.7 fusion.37
  118.3 0.9 fusion.3
  120.8 1.9 collective-permute-start.17
  122.7 2.4 collective-permute-start.14
  125.8 2.5 psum.30
  128.3 34.8 %all-gather.1 = f32[256,64]{1,0:T(8,128)S(1)} all-gather(f32[16,64]{1,0:T(8,128)S(1)} %psum.30), channel_id=3, replica_groups=mesh['gx'=4,'gy'=4,'gz'=2] {'gx','gy'}, dimensions={0}, use_global_device_ids=true | all-gather | bytes 69632 | tf_op jit(solution)/shard_map/all_gather | solution.py:79
  163.1 1.9 collective-permute-start.10
  165.0 4.5 %collective-permute-start.11 = (bf16[16,2,256]{2,0,1:T(8,128)(2,1)}, bf16[16,2,256]{2,0,1:T(8,128)(2,1)}, u32[]{:S(2)}, u32[]{:S(2)}) collective-permute-start(bf16[16,2,256]{2,0,1:T(8,128)(2,1)} %get-tuple-element.11), channel_id=1, source_target_pairs={{1,0},{2,1},{3,2},{4,3},{5,4},{6,5},{7,6},{8,7},{9,8},{10,9},{11,1... | collective-permute-start | bytes 49160 | tf_op jit(solution)/shard_map/ppermute | solution.py:15
  169.6 10.1 %psum.31 = f32[1,16,64]{2,1,0:T(8,128)S(1)} all-reduce(f32[1,16,64]{2,1,0:T(8,128)S(1)} %convolution_bitcast_fusion.7), channel_id=1, replica_groups=mesh['gx'=4,'gy'=4,'gz'=2] {'gy'}, use_global_device_ids=true, to_apply=%region_4.5 | all-reduce | flops 1024 | bytes 8192 | tf_op jit(solution)/shard_map/psum | solution.py:77
  179.7 13.1 %all_gather.15 = f32[4,16,64]{2,1,0:T(8,128)S(1)} all-gather(f32[1,16,64]{2,1,0:T(8,128)S(1)} %psum.31), channel_id=1, replica_groups=mesh['gx'=4,'gy'=4,'gz'=2] {'gx'}, dimensions={0}, use_global_device_ids=true | all-gather | bytes 20480 | tf_op jit(solution)/shard_map/all_gather | solution.py:78
  193.6 1.9 collective-permute-start.12
  197.0 1.9 collective-permute-start.15
  198.9 4.5 %collective-permute-start.18 = (f32[2,16,64]{2,1,0:T(8,128)}, f32[2,16,64]{2,1,0:T(8,128)}, u32[]{:S(2)}, u32[]{:S(2)}) collective-permute-start(f32[2,16,64]{2,1,0:T(8,128)} %get-tuple-element.21), channel_id=1, source_target_pairs={{1,0},{2,1},{3,2},{4,3},{5,4},{6,5},{7,6},{8,7},{9,8},{10,9},{11,1... | collective-permute-start | bytes 24584 | tf_op jit(solution)/shard_map/ppermute | solution.py:15
  203.5 0.8 fusion.17
  204.3 2.0 copy.51
  206.2 11.4 %scatter_custom_fusion = f32[16,4096]{0,1:T(8,128)S(1)} fusion(s32[4096]{0:T(1024)} %get-tuple-element.17, f32[4096,16]{1,0:T(8,128)} %copy.51, f32[]{:T(128)} %constant.15.clone.1), kind=kCustom, calls=%fused_computation.42 | custom fusion | bytes 262656 | tf_op jit(solution)/shard_map/scatter | solution.py:147
  217.7 1.3 copy.58
  218.9 2.4 collective-permute-start.13
  221.4 0.7 pad_maximum_fusion.9
  222.1 1.9 collective-permute-start.16
  224.0 4.7 %collective-permute-start.19 = (f32[3,16,64]{2,1,0:T(8,128)S(1)}, f32[3,16,64]{2,1,0:T(8,128)S(1)}, u32[]{:S(2)}, u32[]{:S(2)}) collective-permute-start(f32[3,16,64]{2,1,0:T(8,128)S(1)} %get-tuple-element.19), channel_id=1, source_target_pairs={{1,0},{2,1},{3,2},{4,3},{5,4},{6,5},{7,6},{8,7},{9,8},{10,9},{11,1... | collective-permute-start | bytes 36872 | tf_op jit(solution)/shard_map/ppermute | solution.py:15
  228.8 0.9 pad_maximum_fusion.3
  230.4 3.8 %convolution_bitcast_fusion = f32[16,16,256]{2,1,0:T(8,128)S(1)} fusion(bf16[16,16,3,256]{3,0,2,1:T(8,128)(2,1)S(1)} %bitcast.177, bf16[16,3,256,256]{3,2,1,0:T(8,128)(2,1)} %param.18), kind=kOutput, calls=%fused_computation.15 | convolution fusion | flops 100663296 | bytes 6946816 | tf_op jit(solution)/shard_map/rlns,lnst->rlt/dot_general | solution.py:101
  234.1 0.8 pad_maximum_fusion.1
  236.5 0.7 fusion.39
  237.2 0.9 fusion.4
  238.3 2.0 copy.57
  240.3 11.4 %scatter_custom_fusion.1 = f32[16,4096]{0,1:T(8,128)S(1)} fusion(s32[4096]{0:T(1024)} %get-tuple-element.17, f32[4096,16]{1,0:T(8,128)} %copy.57, f32[]{:T(128)} %constant.15.clone.1), kind=kCustom, calls=%fused_computation.40 | custom fusion | bytes 262656 | tf_op jit(solution)/shard_map/scatter | solution.py:148
  251.7 1.3 copy.59
  (136 shorter events, 12.8 us)
Async XLA Ops:
  0.6 16.3 %copy-start = (bf16[16,64,256]{2,1,0:T(8,128)(2,1)S(1)}, bf16[16,64,256]{2,1,0:T(8,128)(2,1)}, u32[]{:S(2)}) copy-start(bf16[16,64,256]{2,1,0:T(8,128)(2,1)} %param.20) | copy-start | bytes 1572868
  2.8 14.4 %copy-start.1 = (bf16[16,64,64]{2,1,0:T(8,128)(2,1)S(1)}, bf16[16,64,64]{2,1,0:T(8,128)(2,1)}, u32[]{:S(2)}) copy-start(bf16[16,64,64]{2,1,0:T(8,128)(2,1)} %param.21) | copy-start | bytes 393220
  4.2 26.3 %copy-start.23 = (s32[1,3]{1,0:T(1,128)S(1)}, s32[1,3]{1,0:T(1,128)}, u32[]{:S(2)}) copy-start(s32[1,3]{1,0:T(1,128)} %param.26) | copy-start | bytes 40
  4.3 26.3 %copy-start.24 = (s32[1,3]{1,0:T(1,128)S(1)}, s32[1,3]{1,0:T(1,128)}, u32[]{:S(2)}) copy-start(s32[1,3]{1,0:T(1,128)} %param.29) | copy-start | bytes 40
  4.3 26.4 %copy-start.25 = (s32[1,3]{1,0:T(1,128)S(1)}, s32[1,3]{1,0:T(1,128)}, u32[]{:S(2)}) copy-start(s32[1,3]{1,0:T(1,128)} %param.31) | copy-start | bytes 40
  4.3 26.4 %copy-start.21 = (s32[16,3]{0,1:T(4,128)S(1)}, s32[16,3]{0,1:T(4,128)}, u32[]{:S(2)}) copy-start(s32[16,3]{0,1:T(4,128)} %param.23) | copy-start | bytes 580
  4.3 26.4 %copy-start.22 = (s32[16,3]{0,1:T(4,128)S(1)}, s32[16,3]{0,1:T(4,128)}, u32[]{:S(2)}) copy-start(s32[16,3]{0,1:T(4,128)} %param.19) | copy-start | bytes 580
  4.3 26.6 %copy-start.16 = (bf16[1,64,192]{2,1,0:T(8,128)(2,1)S(1)}, bf16[1,64,192]{2,1,0:T(8,128)(2,1)}, u32[]{:S(2)}) copy-start(bf16[1,64,192]{2,1,0:T(8,128)(2,1)} %param.28) | copy-start | bytes 73732
  4.3 26.7 %copy-start.17 = (bf16[1,64,192]{2,1,0:T(8,128)(2,1)S(1)}, bf16[1,64,192]{2,1,0:T(8,128)(2,1)}, u32[]{:S(2)}) copy-start(bf16[1,64,192]{2,1,0:T(8,128)(2,1)} %param.30) | copy-start | bytes 73732
  4.3 26.8 %copy-start.8 = (bf16[1,64,64]{2,1,0:T(8,128)(2,1)S(1)}, bf16[1,64,64]{2,1,0:T(8,128)(2,1)}, u32[]{:S(2)}) copy-start(bf16[1,64,64]{2,1,0:T(8,128)(2,1)} %param.24) | copy-start | bytes 24580
  4.3 66.1 %copy-start.7 = (bf16[1,64,64]{2,1,0:T(8,128)(2,1)S(1)}, bf16[1,64,64]{2,1,0:T(8,128)(2,1)}, u32[]{:S(2)}) copy-start(bf16[1,64,64]{2,1,0:T(8,128)(2,1)} %param.27) | copy-start | bytes 24580
  16.5 85.9 %copy-start.18 = (bf16[1,64,192]{2,1,0:T(8,128)(2,1)S(1)}, bf16[1,64,192]{2,1,0:T(8,128)(2,1)}, u32[]{:S(2)}) copy-start(bf16[1,64,192]{2,1,0:T(8,128)(2,1)} %param.25) | copy-start | bytes 73732
  16.5 86.0 %copy-start.4 = (bf16[16,64,192]{2,1,0:T(8,128)(2,1)S(1)}, bf16[16,64,192]{2,1,0:T(8,128)(2,1)}, u32[]{:S(2)}) copy-start(bf16[16,64,192]{2,1,0:T(8,128)(2,1)} %param.22) | copy-start | bytes 1179652
  17.4 78.5 %collective-permute-start.7 = (f32[1,16,64]{2,1,0:T(8,128)S(1)}, f32[1,16,64]{2,1,0:T(8,128)S(1)}, u32[]{:S(2)}, u32[]{:S(2)}) collective-permute-start(f32[1,16,64]{2,1,0:T(8,128)S(1)} %bitcast.193), channel_id=1, source_target_pairs={{1,0},{2,1},{3,2},{4,3},{5,4},{6,5},{7,6},{8,7},{9,8},{10,9},{11,1... | collective-permute-start | bytes 12296 | tf_op jit(solution)/shard_map/ppermute | solution.py:15
  20.2 75.7 %collective-permute-start.4 = (f32[1,16,64]{2,1,0:T(8,128)S(1)}, f32[1,16,64]{2,1,0:T(8,128)S(1)}, u32[]{:S(2)}, u32[]{:S(2)}) collective-permute-start(f32[1,16,64]{2,1,0:T(8,128)S(1)} %bitcast.194), channel_id=1, source_target_pairs={{0,1},{1,2},{2,3},{3,4},{4,5},{5,6},{6,7},{7,8},{8,9},{9,10},{10,1... | collective-permute-start | bytes 12296 | tf_op jit(solution)/shard_map/ppermute | solution.py:15
  22.2 85.2 %collective-permute-start = (bf16[16,2,256]{2,0,1:T(8,128)(2,1)S(1)}, bf16[16,2,256]{2,0,1:T(8,128)(2,1)S(1)}, u32[]{:S(2)}, u32[]{:S(2)}) collective-permute-start(bf16[16,2,256]{2,0,1:T(8,128)(2,1)S(1)} %get-tuple-element.14), channel_id=1, source_target_pairs={{0,1},{1,2},{2,3},{3,4},{4,5},{5,6},{6,7},{7,8},{8,9},{9,10},{10,1... | collective-permute-start | bytes 49160 | tf_op jit(solution)/shard_map/ppermute | solution.py:15
  24.8 87.0 %collective-permute-start.1 = (bf16[16,2,256]{2,0,1:T(8,128)(2,1)S(1)}, bf16[16,2,256]{2,0,1:T(8,128)(2,1)S(1)}, u32[]{:S(2)}, u32[]{:S(2)}) collective-permute-start(bf16[16,2,256]{2,0,1:T(8,128)(2,1)S(1)} %get-tuple-element.15), channel_id=1, source_target_pairs={{1,0},{2,1},{3,2},{4,3},{5,4},{6,5},{7,6},{8,7},{9,8},{10,9},{11,1... | collective-permute-start | bytes 49160 | tf_op jit(solution)/shard_map/ppermute | solution.py:15
  28.6 87.5 %collective-permute-start.2 = (f32[16,4,64]{2,0,1:T(8,128)S(1)}, f32[16,4,64]{2,0,1:T(8,128)S(1)}, u32[]{:S(2)}, u32[]{:S(2)}) collective-permute-start(f32[16,4,64]{2,0,1:T(8,128)S(1)} %get-tuple-element.12), channel_id=1, source_target_pairs={{0,1},{1,2},{2,3},{3,4},{4,5},{5,6},{6,7},{7,8},{8,9},{9,10},{10,1... | collective-permute-start | bytes 49160 | tf_op jit(solution)/shard_map/ppermute | solution.py:15
  30.7 86.1 %copy-start.20 = (s32[1024]{0:T(1024)}, s32[1024]{0:T(1024)S(1)}, u32[]{:S(2)}) copy-start(s32[1024]{0:T(1024)S(1)} %pad_clamp_fusion.2) | copy-start | bytes 12292
  95.7 20.5 %copy-start.12 = (s32[1024]{0:T(1024)}, s32[1024]{0:T(1024)S(1)}, u32[]{:S(2)}) copy-start(s32[1024]{0:T(1024)S(1)} %pad_clamp_fusion.3) | copy-start | bytes 12292
  95.9 7.0 %collective-permute-start.5 = (f32[2,16,64]{2,1,0:T(8,128)S(1)}, f32[2,16,64]{2,1,0:T(8,128)S(1)}, u32[]{:S(2)}, u32[]{:S(2)}) collective-permute-start(f32[2,16,64]{2,1,0:T(8,128)S(1)} %get-tuple-element.24), channel_id=1, source_target_pairs={{0,1},{1,2},{2,3},{3,4},{4,5},{5,6},{6,7},{7,8},{8,9},{9,10},{10,1... | collective-permute-start | bytes 24584 | tf_op jit(solution)/shard_map/ppermute | solution.py:15
  97.8 7.4 %collective-permute-start.8 = (f32[2,16,64]{2,1,0:T(8,128)S(1)}, f32[2,16,64]{2,1,0:T(8,128)S(1)}, u32[]{:S(2)}, u32[]{:S(2)}) collective-permute-start(f32[2,16,64]{2,1,0:T(8,128)S(1)} %get-tuple-element.25), channel_id=1, source_target_pairs={{1,0},{2,1},{3,2},{4,3},{5,4},{6,5},{7,6},{8,7},{9,8},{10,9},{11,1... | collective-permute-start | bytes 24584 | tf_op jit(solution)/shard_map/ppermute | solution.py:15
  102.4 13.7 %copy-start.14 = (s32[1024]{0:T(1024)}, s32[1024]{0:T(1024)S(1)}, u32[]{:S(2)}) copy-start(s32[1024]{0:T(1024)S(1)} %pad_clamp_fusion.4) | copy-start | bytes 12292
  102.6 14.9 %copy-start.5 = (bf16[1,64,192]{1,2,0:T(8,128)(2,1)}, bf16[1,64,192]{1,2,0:T(8,128)(2,1)S(1)}, u32[]{:S(2)}) copy-start(bf16[1,64,192]{1,2,0:T(8,128)(2,1)S(1)} %copy.44) | copy-start | bytes 73732
  103.0 13.2 %collective-permute-start.3 = (f32[16,4,64]{2,0,1:T(8,128)S(1)}, f32[16,4,64]{2,0,1:T(8,128)S(1)}, u32[]{:S(2)}, u32[]{:S(2)}) collective-permute-start(f32[16,4,64]{2,0,1:T(8,128)S(1)} %get-tuple-element.13), channel_id=1, source_target_pairs={{1,0},{2,1},{3,2},{4,3},{5,4},{6,5},{7,6},{8,7},{9,8},{10,9},{11,1... | collective-permute-start | bytes 49160 | tf_op jit(solution)/shard_map/ppermute | solution.py:15
  105.3 11.5 %collective-permute-start.6 = (f32[3,16,64]{2,1,0:T(8,128)S(1)}, f32[3,16,64]{2,1,0:T(8,128)S(1)}, u32[]{:S(2)}, u32[]{:S(2)}) collective-permute-start(f32[3,16,64]{2,1,0:T(8,128)S(1)} %get-tuple-element.22), channel_id=1, source_target_pairs={{0,1},{1,2},{2,3},{3,4},{4,5},{5,6},{6,7},{7,8},{8,9},{9,10},{10,1... | collective-permute-start | bytes 36872 | tf_op jit(solution)/shard_map/ppermute | solution.py:15
  107.3 9.5 %collective-permute-start.9 = (f32[3,16,64]{2,1,0:T(8,128)S(1)}, f32[3,16,64]{2,1,0:T(8,128)S(1)}, u32[]{:S(2)}, u32[]{:S(2)}) collective-permute-start(f32[3,16,64]{2,1,0:T(8,128)S(1)} %get-tuple-element.23), channel_id=1, source_target_pairs={{1,0},{2,1},{3,2},{4,3},{5,4},{6,5},{7,6},{8,7},{9,8},{10,9},{11,1... | collective-permute-start | bytes 36872 | tf_op jit(solution)/shard_map/ppermute | solution.py:15
  117.6 3.0 %copy-start.9 = (bf16[1,64,64]{2,1,0:T(8,128)(2,1)S(1)}, bf16[1,64,64]{2,1,0:T(8,128)(2,1)}, u32[]{:S(2)}) copy-start(bf16[1,64,64]{2,1,0:T(8,128)(2,1)} %param.24) | copy-start | bytes 24580
  119.5 86.8 %copy-start.3 = (bf16[16,16,256]{2,0,1:T(8,128)(2,1)}, bf16[16,16,256]{2,0,1:T(8,128)(2,1)S(1)}, u32[]{:S(2)}) copy-start(bf16[16,16,256]{2,0,1:T(8,128)(2,1)S(1)} %get-tuple-element.26) | copy-start | bytes 393220
  120.6 83.6 %copy-start.10 = (f32[16,64,1]{1,0,2:T(8,128)}, f32[16,64,1]{1,0,2:T(8,128)S(1)}, u32[]{:S(2)}) copy-start(f32[16,64,1]{1,0,2:T(8,128)S(1)} %fusion.38) | copy-start | bytes 12292
  120.8 75.6 %collective-permute-start.17 = (f32[1,16,64]{2,1,0:T(8,128)S(1)}, f32[1,16,64]{2,1,0:T(8,128)S(1)}, u32[]{:S(2)}, u32[]{:S(2)}) collective-permute-start(f32[1,16,64]{2,1,0:T(8,128)S(1)} %bitcast.197), channel_id=1, source_target_pairs={{1,0},{2,1},{3,2},{4,3},{5,4},{6,5},{7,6},{8,7},{9,8},{10,9},{11,1... | collective-permute-start | bytes 12296 | tf_op jit(solution)/shard_map/ppermute | solution.py:15
  122.7 73.7 %collective-permute-start.14 = (f32[1,16,64]{2,1,0:T(8,128)S(1)}, f32[1,16,64]{2,1,0:T(8,128)S(1)}, u32[]{:S(2)}, u32[]{:S(2)}) collective-permute-start(f32[1,16,64]{2,1,0:T(8,128)S(1)} %bitcast.198), channel_id=1, source_target_pairs={{0,1},{1,2},{2,3},{3,4},{4,5},{5,6},{6,7},{7,8},{8,9},{9,10},{10,1... | collective-permute-start | bytes 12296 | tf_op jit(solution)/shard_map/ppermute | solution.py:15
  163.1 60.9 %collective-permute-start.10 = (bf16[16,2,256]{2,0,1:T(8,128)(2,1)}, bf16[16,2,256]{2,0,1:T(8,128)(2,1)}, u32[]{:S(2)}, u32[]{:S(2)}) collective-permute-start(bf16[16,2,256]{2,0,1:T(8,128)(2,1)} %get-tuple-element.10), channel_id=1, source_target_pairs={{0,1},{1,2},{2,3},{3,4},{4,5},{5,6},{6,7},{7,8},{8,9},{9,10},{10,1... | collective-permute-start | bytes 49160 | tf_op jit(solution)/shard_map/ppermute | solution.py:15
  165.0 63.8 %collective-permute-start.11 = (bf16[16,2,256]{2,0,1:T(8,128)(2,1)}, bf16[16,2,256]{2,0,1:T(8,128)(2,1)}, u32[]{:S(2)}, u32[]{:S(2)}) collective-permute-start(bf16[16,2,256]{2,0,1:T(8,128)(2,1)} %get-tuple-element.11), channel_id=1, source_target_pairs={{1,0},{2,1},{3,2},{4,3},{5,4},{6,5},{7,6},{8,7},{9,8},{10,9},{11,1... | collective-permute-start | bytes 49160 | tf_op jit(solution)/shard_map/ppermute | solution.py:15
  193.6 40.5 %collective-permute-start.12 = (f32[16,4,64]{2,0,1:T(8,128)}, f32[16,4,64]{2,0,1:T(8,128)}, u32[]{:S(2)}, u32[]{:S(2)}) collective-permute-start(f32[16,4,64]{2,0,1:T(8,128)} %get-tuple-element.8), channel_id=1, source_target_pairs={{0,1},{1,2},{2,3},{3,4},{4,5},{5,6},{6,7},{7,8},{8,9},{9,10},{10,1... | collective-permute-start | bytes 49160 | tf_op jit(solution)/shard_map/ppermute | solution.py:15
  197.0 21.9 %collective-permute-start.15 = (f32[2,16,64]{2,1,0:T(8,128)}, f32[2,16,64]{2,1,0:T(8,128)}, u32[]{:S(2)}, u32[]{:S(2)}) collective-permute-start(f32[2,16,64]{2,1,0:T(8,128)} %get-tuple-element.20), channel_id=1, source_target_pairs={{0,1},{1,2},{2,3},{3,4},{4,5},{5,6},{6,7},{7,8},{8,9},{9,10},{10,1... | collective-permute-start | bytes 24584 | tf_op jit(solution)/shard_map/ppermute | solution.py:15
  198.9 22.4 %collective-permute-start.18 = (f32[2,16,64]{2,1,0:T(8,128)}, f32[2,16,64]{2,1,0:T(8,128)}, u32[]{:S(2)}, u32[]{:S(2)}) collective-permute-start(f32[2,16,64]{2,1,0:T(8,128)} %get-tuple-element.21), channel_id=1, source_target_pairs={{1,0},{2,1},{3,2},{4,3},{5,4},{6,5},{7,6},{8,7},{9,8},{10,9},{11,1... | collective-permute-start | bytes 24584 | tf_op jit(solution)/shard_map/ppermute | solution.py:15
  206.2 15.1 %copy-start.11 = (f32[16,64,1]{1,0,2:T(8,128)S(1)}, f32[16,64,1]{1,0,2:T(8,128)}, u32[]{:S(2)}) copy-start(f32[16,64,1]{1,0,2:T(8,128)} %copy-done.10) | copy-start | bytes 12292
  206.2 23.5 %copy-start.15 = (s32[1024]{0:T(1024)S(1)}, s32[1024]{0:T(1024)}, u32[]{:S(2)}) copy-start(s32[1024]{0:T(1024)} %copy-done.14) | copy-start | bytes 12292
  218.9 15.2 %collective-permute-start.13 = (f32[16,4,64]{2,0,1:T(8,128)}, f32[16,4,64]{2,0,1:T(8,128)S(1)}, u32[]{:S(2)}, u32[]{:S(2)}) collective-permute-start(f32[16,4,64]{2,0,1:T(8,128)} %get-tuple-element.9), channel_id=1, source_target_pairs={{1,0},{2,1},{3,2},{4,3},{5,4},{6,5},{7,6},{8,7},{9,8},{10,9},{11,1... | collective-permute-start | bytes 49160 | tf_op jit(solution)/shard_map/ppermute | solution.py:15
  222.1 13.4 %collective-permute-start.16 = (f32[3,16,64]{2,1,0:T(8,128)S(1)}, f32[3,16,64]{2,1,0:T(8,128)S(1)}, u32[]{:S(2)}, u32[]{:S(2)}) collective-permute-start(f32[3,16,64]{2,1,0:T(8,128)S(1)} %get-tuple-element.18), channel_id=1, source_target_pairs={{0,1},{1,2},{2,3},{3,4},{4,5},{5,6},{6,7},{7,8},{8,9},{9,10},{10,1... | collective-permute-start | bytes 36872 | tf_op jit(solution)/shard_map/ppermute | solution.py:15
  224.0 11.5 %collective-permute-start.19 = (f32[3,16,64]{2,1,0:T(8,128)S(1)}, f32[3,16,64]{2,1,0:T(8,128)S(1)}, u32[]{:S(2)}, u32[]{:S(2)}) collective-permute-start(f32[3,16,64]{2,1,0:T(8,128)S(1)} %get-tuple-element.19), channel_id=1, source_target_pairs={{1,0},{2,1},{3,2},{4,3},{5,4},{6,5},{7,6},{8,7},{9,8},{10,9},{11,1... | collective-permute-start | bytes 36872 | tf_op jit(solution)/shard_map/ppermute | solution.py:15
  230.3 4.6 %copy-start.13 = (s32[1024]{0:T(1024)S(1)}, s32[1024]{0:T(1024)}, u32[]{:S(2)}) copy-start(s32[1024]{0:T(1024)} %copy-done.12) | copy-start | bytes 12292
  230.3 5.9 %copy-start.6 = (bf16[1,64,192]{1,2,0:T(8,128)(2,1)S(1)}, bf16[1,64,192]{1,2,0:T(8,128)(2,1)}, u32[]{:S(2)}) copy-start(bf16[1,64,192]{1,2,0:T(8,128)(2,1)} %copy-done.5) | copy-start | bytes 73732
  230.3 5.9 %copy-start.19 = (f32[16,64]{1,0:T(8,128)S(1)}, f32[16,64]{1,0:T(8,128)}, u32[]{:S(2)}) copy-start(f32[16,64]{1,0:T(8,128)} %fusion.17) | copy-start | bytes 12292
  230.4 6.1 %copy-start.2 = (bf16[16,64,64]{2,1,0:T(8,128)(2,1)S(1)}, bf16[16,64,64]{2,1,0:T(8,128)(2,1)}, u32[]{:S(2)}) copy-start(bf16[16,64,64]{2,1,0:T(8,128)(2,1)} %param.21) | copy-start | bytes 393220
where the time goes:
time: 254 us; the launch traced here: 253 us
  blocking collectives  123 us (48%)
  starting transfers between devices  56.5 us (22%)
  local copies, waits for them, and re-layouts  51.6 us (20%)
  matrix products  14.8 us (6%)
  other arithmetic  5.39 us (2%)
    all_gather x2, blocking collectives, apply_matrix(): lax.all_gather(block_moment[None], ('gx', 'gy'), axis=0, tiled=True)  70.3 us
    ppermute x20, starting transfers between devices, shifted(): return lax.ppermute(block, axis, route)  56.5 us
    all_gather x2, blocking collectives, apply_matrix(): every_top = lax.all_gather(top_moment[None], 'gx', axis=0, tiled=True)  26.3 us
    psum x2, blocking collectives, apply_matrix(): top_moment = lax.psum(top_term, 'gy')  20.4 us
    gather x2, local copies, waits for them, and re-layouts, shards(): jnp.take(signal, order, axis=1).astype(jnp.bfloat16)  12.4 us
    scatter x1, local copies, waits for them, and re-layouts, shards(): smoothed = empty.at[:, order].set(first.reshape(rhs_count, -1))  11.4 us
    scatter x1, local copies, waits for them, and re-layouts, shards(): twice = empty.at[:, order].set(second.reshape(rhs_count, -1))  11.4 us
    dot_general x2, matrix products, apply_matrix(): jnp.einsum('rlns,lnst->rlt', near_rows, near_tiles, preferred_element_typ...  7.46 us
  transfers between devices with their start and end apart: 20, of which 0 were waited for; matrix products, arithmetic and copies ran while one was open for 13% of the time, Pallas kernels for 0%

commit v1 on v0

--- a/solution.py
+++ b/solution.py
@@ -7,6 +7,14 @@
 LINK_REACH = 4
 DEVICE_REACH = 3
 HIGH = lax.Precision.HIGHEST
+
+
+def doubling_sum(array, axis):
+    peers, acc = (lax.axis_size(axis), array)
+    for stride in [1 << k for k in range(peers.bit_length() - 1)]:
+        swap = [(i, i ^ stride) for i in range(peers)]
+        acc = acc + lax.ppermute(acc, axis, swap)
+    return acc
 
 
 def shifted(block, axis, distance):
@@ -74,7 +82,7 @@
     position = relative + DEVICE_REACH - (relative > 0).astype(jnp.int32)
     device_picked = stacked[position]
     top_term = jnp.dot(block_moment, block_transfer[0].astype(jnp.float32), precision=HIGH)
-    top_moment = lax.psum(top_term, "gy")
+    top_moment = doubling_sum(top_term, "gy")
     every_top = lax.all_gather(top_moment[None], "gx", axis=0, tiled=True)
     every_block = lax.all_gather(block_moment[None], ("gx", "gy"), axis=0, tiled=True)
     top_field = couple(every_top[top_links[0]], top_coupling[0])

time: 254 us -> 245 us (0.965)
  blocking collectives: 123 us -> 103 us
  starting transfers between devices: 56.5 us -> 62.8 us
  matrix products: 14.8 us -> 18.9 us
    psum x2 -> x0, blocking collectives: 20.4 us -> none  [apply_matrix(): top_moment = lax.psum(top_term, 'gy')]
    ppermute x0 -> x4, starting transfers between devices: none -> 7.17 us  [doubling_sum(): acc = acc + lax.ppermute(acc, axis, swap)]
  transfers between devices with their start and end apart: 20 -> 24, of which waited for: 0 -> 0; matrix products, arithmetic and copies ran while one was open for 13% -> 15% of each run, Pallas kernels for 0% -> 0%
where the time goes in v1:
time: 245 us; the launch traced here: 244 us
  blocking collectives  103 us (42%)
  starting transfers between devices  62.8 us (26%)
  local copies, waits for them, and re-layouts  51.7 us (21%)
  matrix products  18.9 us (8%)
  other arithmetic  5.41 us (2%)
    all_gather x2, blocking collectives, apply_matrix(): lax.all_gather(block_moment[None], ('gx', 'gy'), axis=0, tiled=True)  71.7 us
    ppermute x20, starting transfers between devices, shifted(): return lax.ppermute(block, axis, route)  55.7 us
    all_gather x2, blocking collectives, apply_matrix(): every_top = lax.all_gather(top_moment[None], 'gx', axis=0, tiled=True)  26.3 us
    gather x2, local copies, waits for them, and re-layouts, shards(): jnp.take(signal, order, axis=1).astype(jnp.bfloat16)  12.4 us
    scatter x1, local copies, waits for them, and re-layouts, shards(): smoothed = empty.at[:, order].set(first.reshape(rhs_count, -1))  11.4 us
    scatter x1, local copies, waits for them, and re-layouts, shards(): twice = empty.at[:, order].set(second.reshape(rhs_count, -1))  11.4 us
    dot_general x2, matrix products, apply_matrix(): jnp.einsum('rlns,lnst->rlt', near_rows, near_tiles, preferred_element_typ...  7.46 us
    ppermute x4, starting transfers between devices, doubling_sum(): acc = acc + lax.ppermute(acc, axis, swap)  7.17 us
  transfers between devices with their start and end apart: 24, of which 0 were waited for; matrix products, arithmetic and copies ran while one was open for 15% of the time, Pallas kernels for 0%

profile of v1, /device:TPU:4, one launch (start us, length us, event | category | flops | bytes accessed | tf_op | source)
XLA Modules:
  0.0 243.5 jit_solution(1954102983093475536)
XLA Ops:
  1.4 1.3 broadcast_clamp_fusion
  2.8 1.5 copy.24
  4.4 12.1 %gather_fusion = bf16[4096,16]{1,0:T(8,128)(2,1)S(1)} fusion(bf16[16,4096]{0,1:T(8,128)(2,1)S(1)} %copy.24, s32[4096]{0:T(1024)S(1)} %get-tuple-element.14), kind=kCustom, calls=%fused_computation | custom fusion | bytes 278528 | tf_op jit(solution)/shard_map/jit(_take)/gather | solution.py:151
  17.4 2.8 %collective-permute-start.7 = (f32[1,16,64]{2,1,0:T(8,128)S(1)}, f32[1,16,64]{2,1,0:T(8,128)S(1)}, u32[]{:S(2)}, u32[]{:S(2)}) collective-permute-start(f32[1,16,64]{2,1,0:T(8,128)S(1)} %bitcast.191), channel_id=1, source_target_pairs={{1,0},{2,1},{3,2},{4,3},{5,4},{6,5},{7,6},{8,7},{9,8},{10,9},{11,1... | collective-permute-start | bytes 12296 | tf_op jit(solution)/shard_map/ppermute | solution.py:23
  20.2 1.9 collective-permute-start.4
  22.1 2.6 %collective-permute-start = (bf16[16,2,256]{2,0,1:T(8,128)(2,1)S(1)}, bf16[16,2,256]{2,0,1:T(8,128)(2,1)S(1)}, u32[]{:S(2)}, u32[]{:S(2)}) collective-permute-start(bf16[16,2,256]{2,0,1:T(8,128)(2,1)S(1)} %get-tuple-element.12), channel_id=1, source_target_pairs={{0,1},{1,2},{2,3},{3,4},{4,5},{5,6},{6,7},{7,8},{8,9},{9,10},{10,1... | collective-permute-start | bytes 49160 | tf_op jit(solution)/shard_map/ppermute | solution.py:23
  24.8 3.8 %collective-permute-start.1 = (bf16[16,2,256]{2,0,1:T(8,128)(2,1)S(1)}, bf16[16,2,256]{2,0,1:T(8,128)(2,1)S(1)}, u32[]{:S(2)}, u32[]{:S(2)}) collective-permute-start(bf16[16,2,256]{2,0,1:T(8,128)(2,1)S(1)} %get-tuple-element.13), channel_id=1, source_target_pairs={{1,0},{2,1},{3,2},{4,3},{5,4},{6,5},{7,6},{8,7},{9,8},{10,9},{11,1... | collective-permute-start | bytes 49160 | tf_op jit(solution)/shard_map/ppermute | solution.py:23
  28.8 2.5 %psum.14 = f32[16,64]{1,0:T(8,128)S(1)} all-reduce(f32[16,64]{1,0:T(8,128)S(1)} %fusion.25), channel_id=1, replica_groups=mesh['gx'=4,'gy'=4,'gz'=2] {'gz'}, use_global_device_ids=true, to_apply=%region_0.1 | all-reduce | flops 1024 | bytes 8192 | tf_op jit(solution)/shard_map/psum | solution.py:77
  31.4 1.5 collective-permute-start.10
  32.9 37.0 %all-gather = f32[256,64]{1,0:T(8,128)S(1)} all-gather(f32[16,64]{1,0:T(8,128)S(1)} %psum.14), channel_id=2, replica_groups=mesh['gx'=4,'gy'=4,'gz'=2] {'gx','gy'}, dimensions={0}, use_global_device_ids=true | all-gather | bytes 69632 | tf_op jit(solution)/shard_map/all_gather | solution.py:87
  72.0 1.9 collective-permute-start.2
  73.9 3.6 %collective-permute-start.11 = (f32[16,64]{1,0:T(8,128)S(1)}, f32[16,64]{1,0:T(8,128)S(1)}, u32[]{:S(2)}, u32[]{:S(2)}) collective-permute-start(f32[16,64]{1,0:T(8,128)S(1)} %add.143), channel_id=1, source_target_pairs={{0,4},{2,6},{4,0},{6,2},{1,5},{3,7},{5,1},{7,3},{8,12},{10,14},{12... | collective-permute-start | bytes 12296 | tf_op jit(solution)/shard_map/ppermute | solution.py:16
  77.5 1.9 collective-permute-start.5
  79.5 4.5 %collective-permute-start.8 = (f32[2,16,64]{2,1,0:T(8,128)S(1)}, f32[2,16,64]{2,1,0:T(8,128)S(1)}, u32[]{:S(2)}, u32[]{:S(2)}) collective-permute-start(f32[2,16,64]{2,1,0:T(8,128)S(1)} %get-tuple-element.23), channel_id=1, source_target_pairs={{1,0},{2,1},{3,2},{4,3},{5,4},{6,5},{7,6},{8,7},{9,8},{10,9},{11,1... | collective-permute-start | bytes 24584 | tf_op jit(solution)/shard_map/ppermute | solution.py:23
  84.0 13.1 %all-gather.1 = f32[64,64]{1,0:T(8,128)S(1)} all-gather(f32[16,64]{1,0:T(8,128)S(1)} %add.144), channel_id=3, replica_groups=mesh['gx'=4,'gy'=4,'gz'=2] {'gx'}, dimensions={0}, use_global_device_ids=true | all-gather | bytes 20480 | tf_op jit(solution)/shard_map/all_gather | solution.py:86
  98.2 2.0 collective-permute-start.3
  100.2 2.4 collective-permute-start.6
  102.6 4.1 %collective-permute-start.9 = (f32[3,16,64]{2,1,0:T(8,128)S(1)}, f32[3,16,64]{2,1,0:T(8,128)S(1)}, u32[]{:S(2)}, u32[]{:S(2)}) collective-permute-start(f32[3,16,64]{2,1,0:T(8,128)S(1)} %get-tuple-element.21), channel_id=1, source_target_pairs={{1,0},{2,1},{3,2},{4,3},{5,4},{6,5},{7,6},{8,7},{9,8},{10,9},{11,1... | collective-permute-start | bytes 36872 | tf_op jit(solution)/shard_map/ppermute | solution.py:23
  107.3 3.7 %convolution_bitcast_fusion.1 = f32[16,16,256]{2,1,0:T(8,128)S(1)} fusion(bf16[16,16,3,256]{3,0,2,1:T(8,128)(2,1)S(1)} %bitcast.176, bf16[16,3,256,256]{3,2,1,0:T(8,128)(2,1)} %param.18), kind=kOutput, calls=%fused_computation.17 | convolution fusion | flops 100663296 | bytes 6946816 | tf_op jit(solution)/shard_map/rlns,lnst->rlt/dot_general | solution.py:109
  113.2 0.9 fusion.3
  115.2 0.9 fusion.40
  116.1 0.8 fusion.21
  116.9 1.9 collective-permute-start.19
  118.9 2.4 collective-permute-start.16
  121.9 2.5 %psum.15 = f32[16,64]{1,0:T(8,128)S(1)} all-reduce(f32[16,64]{1,0:T(8,128)S(1)} %fusion.21), channel_id=1, replica_groups=mesh['gx'=4,'gy'=4,'gz'=2] {'gz'}, use_global_device_ids=true, to_apply=%region_2.3 | all-reduce | flops 1024 | bytes 8192 | tf_op jit(solution)/shard_map/psum | solution.py:77
  125.1 34.7 %all-gather.2 = f32[256,64]{1,0:T(8,128)S(1)} all-gather(f32[16,64]{1,0:T(8,128)S(1)} %psum.15), channel_id=4, replica_groups=mesh['gx'=4,'gy'=4,'gz'=2] {'gx','gy'}, dimensions={0}, use_global_device_ids=true | all-gather | bytes 69632 | tf_op jit(solution)/shard_map/all_gather | solution.py:87
  159.8 1.9 collective-permute-start.12
  161.7 4.5 %collective-permute-start.13 = (bf16[16,2,256]{2,0,1:T(8,128)(2,1)}, bf16[16,2,256]{2,0,1:T(8,128)(2,1)}, u32[]{:S(2)}, u32[]{:S(2)}) collective-permute-start(bf16[16,2,256]{2,0,1:T(8,128)(2,1)} %get-tuple-element.9), channel_id=1, source_target_pairs={{1,0},{2,1},{3,2},{4,3},{5,4},{6,5},{7,6},{8,7},{9,8},{10,9},{11,1... | collective-permute-start | bytes 49160 | tf_op jit(solution)/shard_map/ppermute | solution.py:23
  167.7 1.9 copy.33
  169.6 11.4 %scatter_custom_fusion = f32[16,4096]{0,1:T(8,128)S(1)} fusion(s32[4096]{0:T(1024)} %get-tuple-element.15, f32[4096,16]{1,0:T(8,128)} %copy.33, f32[]{:T(128)} %constant.15.clone.1), kind=kCustom, calls=%fused_computation.40 | custom fusion | bytes 262656 | tf_op jit(solution)/shard_map/scatter | solution.py:155
  181.1 1.3 copy.36
  182.3 1.9 collective-permute-start.14
  185.0 2.0 collective-permute-start.23
  187.7 2.6 %collective-permute-start.17 = (f32[2,16,64]{2,1,0:T(8,128)S(1)}, f32[2,16,64]{2,1,0:T(8,128)S(1)}, u32[]{:S(2)}, u32[]{:S(2)}) collective-permute-start(f32[2,16,64]{2,1,0:T(8,128)S(1)} %get-tuple-element.18), channel_id=1, source_target_pairs={{0,1},{1,2},{2,3},{3,4},{4,5},{5,6},{6,7},{7,8},{8,9},{9,10},{10,1... | collective-permute-start | bytes 24584 | tf_op jit(solution)/shard_map/ppermute | solution.py:23
  190.3 3.8 %collective-permute-start.20 = (f32[2,16,64]{2,1,0:T(8,128)S(1)}, f32[2,16,64]{2,1,0:T(8,128)S(1)}, u32[]{:S(2)}, u32[]{:S(2)}) collective-permute-start(f32[2,16,64]{2,1,0:T(8,128)S(1)} %get-tuple-element.19), channel_id=1, source_target_pairs={{1,0},{2,1},{3,2},{4,3},{5,4},{6,5},{7,6},{8,7},{9,8},{10,9},{11,1... | collective-permute-start | bytes 24584 | tf_op jit(solution)/shard_map/ppermute | solution.py:23
  194.2 13.1 %all-gather.3 = f32[64,64]{1,0:T(8,128)S(1)} all-gather(f32[16,64]{1,0:T(8,128)S(1)} %add.152), channel_id=5, replica_groups=mesh['gx'=4,'gy'=4,'gz'=2] {'gx'}, dimensions={0}, use_global_device_ids=true | all-gather | bytes 20480 | tf_op jit(solution)/shard_map/all_gather | solution.py:86
  208.0 1.0 convolution_bitcast_fusion.6
  209.0 0.8 convolution_add_fusion.2
  209.8 0.9 fusion.19
  210.7 1.9 collective-permute-start.15
  213.3 2.4 collective-permute-start.18
  215.7 4.2 %collective-permute-start.21 = (f32[3,16,64]{2,1,0:T(8,128)S(1)}, f32[3,16,64]{2,1,0:T(8,128)S(1)}, u32[]{:S(2)}, u32[]{:S(2)}) collective-permute-start(f32[3,16,64]{2,1,0:T(8,128)S(1)} %get-tuple-element.17), channel_id=1, source_target_pairs={{1,0},{2,1},{3,2},{4,3},{5,4},{6,5},{7,6},{8,7},{9,8},{10,9},{11,1... | collective-permute-start | bytes 36872 | tf_op jit(solution)/shard_map/ppermute | solution.py:23
  220.0 0.9 pad_maximum_fusion.3
  221.7 3.8 %convolution_bitcast_fusion = f32[16,16,256]{2,1,0:T(8,128)S(1)} fusion(bf16[16,16,3,256]{3,0,2,1:T(8,128)(2,1)S(1)} %bitcast.175, bf16[16,3,256,256]{3,2,1,0:T(8,128)(2,1)} %param.18), kind=kOutput, calls=%fused_computation.15 | convolution fusion | flops 100663296 | bytes 6946816 | tf_op jit(solution)/shard_map/rlns,lnst->rlt/dot_general | solution.py:109
  227.7 0.9 fusion.4
  228.9 1.9 copy.35
  230.8 11.4 %scatter_custom_fusion.1 = f32[16,4096]{0,1:T(8,128)S(1)} fusion(s32[4096]{0:T(1024)} %get-tuple-element.15, f32[4096,16]{1,0:T(8,128)} %copy.35, f32[]{:T(128)} %constant.15.clone.1), kind=kCustom, calls=%fused_computation.38 | custom fusion | bytes 262656 | tf_op jit(solution)/shard_map/scatter | solution.py:156
  242.3 1.3 copy.37
  (142 shorter events, 17.4 us)
Async XLA Ops:
  0.6 16.3 %copy-start = (bf16[16,64,256]{2,1,0:T(8,128)(2,1)S(1)}, bf16[16,64,256]{2,1,0:T(8,128)(2,1)}, u32[]{:S(2)}) copy-start(bf16[16,64,256]{2,1,0:T(8,128)(2,1)} %param.20) | copy-start | bytes 1572868
  2.8 14.4 %copy-start.1 = (bf16[16,64,64]{2,1,0:T(8,128)(2,1)S(1)}, bf16[16,64,64]{2,1,0:T(8,128)(2,1)}, u32[]{:S(2)}) copy-start(bf16[16,64,64]{2,1,0:T(8,128)(2,1)} %param.21) | copy-start | bytes 393220
  4.2 24.4 %copy-start.9 = (bf16[1,64,64]{2,1,0:T(8,128)(2,1)S(1)}, bf16[1,64,64]{2,1,0:T(8,128)(2,1)}, u32[]{:S(2)}) copy-start(bf16[1,64,64]{2,1,0:T(8,128)(2,1)} %param.24) | copy-start | bytes 24580
  4.3 27.0 %copy-start.8 = (bf16[1,64,64]{2,1,0:T(8,128)(2,1)S(1)}, bf16[1,64,64]{2,1,0:T(8,128)(2,1)}, u32[]{:S(2)}) copy-start(bf16[1,64,64]{2,1,0:T(8,128)(2,1)} %param.27) | copy-start | bytes 24580
  4.3 65.6 %copy-start.21 = (s32[1,3]{1,0:T(1,128)S(1)}, s32[1,3]{1,0:T(1,128)}, u32[]{:S(2)}) copy-start(s32[1,3]{1,0:T(1,128)} %param.26) | copy-start | bytes 40
  4.3 65.6 %copy-start.22 = (s32[1,3]{1,0:T(1,128)S(1)}, s32[1,3]{1,0:T(1,128)}, u32[]{:S(2)}) copy-start(s32[1,3]{1,0:T(1,128)} %param.29) | copy-start | bytes 40
  4.3 65.6 %copy-start.23 = (s32[1,3]{1,0:T(1,128)S(1)}, s32[1,3]{1,0:T(1,128)}, u32[]{:S(2)}) copy-start(s32[1,3]{1,0:T(1,128)} %param.31) | copy-start | bytes 40
  4.3 65.7 %copy-start.19 = (s32[16,3]{0,1:T(4,128)S(1)}, s32[16,3]{0,1:T(4,128)}, u32[]{:S(2)}) copy-start(s32[16,3]{0,1:T(4,128)} %param.23) | copy-start | bytes 580
  4.3 65.7 %copy-start.20 = (s32[16,3]{0,1:T(4,128)S(1)}, s32[16,3]{0,1:T(4,128)}, u32[]{:S(2)}) copy-start(s32[16,3]{0,1:T(4,128)} %param.19) | copy-start | bytes 580
  4.3 66.1 %copy-start.14 = (bf16[1,64,192]{2,1,0:T(8,128)(2,1)S(1)}, bf16[1,64,192]{2,1,0:T(8,128)(2,1)}, u32[]{:S(2)}) copy-start(bf16[1,64,192]{2,1,0:T(8,128)(2,1)} %param.28) | copy-start | bytes 73732
  4.3 66.9 %copy-start.15 = (bf16[1,64,192]{2,1,0:T(8,128)(2,1)S(1)}, bf16[1,64,192]{2,1,0:T(8,128)(2,1)}, u32[]{:S(2)}) copy-start(bf16[1,64,192]{2,1,0:T(8,128)(2,1)} %param.25) | copy-start | bytes 73732
  4.4 67.1 %copy-start.16 = (bf16[1,64,192]{2,1,0:T(8,128)(2,1)S(1)}, bf16[1,64,192]{2,1,0:T(8,128)(2,1)}, u32[]{:S(2)}) copy-start(bf16[1,64,192]{2,1,0:T(8,128)(2,1)} %param.30) | copy-start | bytes 73732
  16.5 55.0 %copy-start.4 = (bf16[16,64,192]{2,1,0:T(8,128)(2,1)S(1)}, bf16[16,64,192]{2,1,0:T(8,128)(2,1)}, u32[]{:S(2)}) copy-start(bf16[16,64,192]{2,1,0:T(8,128)(2,1)} %param.22) | copy-start | bytes 1179652
  17.4 56.5 %collective-permute-start.7 = (f32[1,16,64]{2,1,0:T(8,128)S(1)}, f32[1,16,64]{2,1,0:T(8,128)S(1)}, u32[]{:S(2)}, u32[]{:S(2)}) collective-permute-start(f32[1,16,64]{2,1,0:T(8,128)S(1)} %bitcast.191), channel_id=1, source_target_pairs={{1,0},{2,1},{3,2},{4,3},{5,4},{6,5},{7,6},{8,7},{9,8},{10,9},{11,1... | collective-permute-start | bytes 12296 | tf_op jit(solution)/shard_map/ppermute | solution.py:23
  20.2 57.3 %collective-permute-start.4 = (f32[1,16,64]{2,1,0:T(8,128)S(1)}, f32[1,16,64]{2,1,0:T(8,128)S(1)}, u32[]{:S(2)}, u32[]{:S(2)}) collective-permute-start(f32[1,16,64]{2,1,0:T(8,128)S(1)} %bitcast.192), channel_id=1, source_target_pairs={{0,1},{1,2},{2,3},{3,4},{4,5},{5,6},{6,7},{7,8},{8,9},{9,10},{10,1... | collective-permute-start | bytes 12296 | tf_op jit(solution)/shard_map/ppermute | solution.py:23
  22.1 80.4 %collective-permute-start = (bf16[16,2,256]{2,0,1:T(8,128)(2,1)S(1)}, bf16[16,2,256]{2,0,1:T(8,128)(2,1)S(1)}, u32[]{:S(2)}, u32[]{:S(2)}) collective-permute-start(bf16[16,2,256]{2,0,1:T(8,128)(2,1)S(1)} %get-tuple-element.12), channel_id=1, source_target_pairs={{0,1},{1,2},{2,3},{3,4},{4,5},{5,6},{6,7},{7,8},{8,9},{9,10},{10,1... | collective-permute-start | bytes 49160 | tf_op jit(solution)/shard_map/ppermute | solution.py:23
  24.8 81.8 %collective-permute-start.1 = (bf16[16,2,256]{2,0,1:T(8,128)(2,1)S(1)}, bf16[16,2,256]{2,0,1:T(8,128)(2,1)S(1)}, u32[]{:S(2)}, u32[]{:S(2)}) collective-permute-start(bf16[16,2,256]{2,0,1:T(8,128)(2,1)S(1)} %get-tuple-element.13), channel_id=1, source_target_pairs={{1,0},{2,1},{3,2},{4,3},{5,4},{6,5},{7,6},{8,7},{9,8},{10,9},{11,1... | collective-permute-start | bytes 49160 | tf_op jit(solution)/shard_map/ppermute | solution.py:23
  31.4 40.6 %collective-permute-start.10 = (f32[16,64]{1,0:T(8,128)S(1)}, f32[16,64]{1,0:T(8,128)S(1)}, u32[]{:S(2)}, u32[]{:S(2)}) collective-permute-start(f32[16,64]{1,0:T(8,128)S(1)} %fusion.17), channel_id=1, source_target_pairs={{0,2},{2,0},{4,6},{6,4},{1,3},{3,1},{5,7},{7,5},{8,10},{10,8},{12,... | collective-permute-start | bytes 12296 | tf_op jit(solution)/shard_map/ppermute | solution.py:16
  70.0 41.0 %copy-start.18 = (s32[1024]{0:T(1024)}, s32[1024]{0:T(1024)S(1)}, u32[]{:S(2)}) copy-start(s32[1024]{0:T(1024)S(1)} %pad_clamp_fusion) | copy-start | bytes 12292
  70.0 41.7 %copy-start.17 = (s32[1024]{0:T(1024)}, s32[1024]{0:T(1024)S(1)}, u32[]{:S(2)}) copy-start(s32[1024]{0:T(1024)S(1)} %pad_clamp_fusion.2) | copy-start | bytes 12292
  70.2 40.8 %copy-start.11 = (s32[1024]{0:T(1024)}, s32[1024]{0:T(1024)S(1)}, u32[]{:S(2)}) copy-start(s32[1024]{0:T(1024)S(1)} %pad_clamp_fusion.3) | copy-start | bytes 12292
  71.3 39.7 %copy-start.13 = (s32[1024]{0:T(1024)}, s32[1024]{0:T(1024)S(1)}, u32[]{:S(2)}) copy-start(s32[1024]{0:T(1024)S(1)} %pad_clamp_fusion.4) | copy-start | bytes 12292
  71.4 40.9 %copy-start.6 = (bf16[1,64,192]{1,2,0:T(8,128)(2,1)}, bf16[1,64,192]{1,2,0:T(8,128)(2,1)S(1)}, u32[]{:S(2)}) copy-start(bf16[1,64,192]{1,2,0:T(8,128)(2,1)S(1)} %copy.29) | copy-start | bytes 73732
  71.5 39.4 %copy-start.5 = (bf16[1,64,192]{1,2,0:T(8,128)(2,1)}, bf16[1,64,192]{1,2,0:T(8,128)(2,1)S(1)}, u32[]{:S(2)}) copy-start(bf16[1,64,192]{1,2,0:T(8,128)(2,1)S(1)} %copy.31) | copy-start | bytes 73732
  72.0 39.0 %collective-permute-start.2 = (f32[16,4,64]{2,0,1:T(8,128)S(1)}, f32[16,4,64]{2,0,1:T(8,128)S(1)}, u32[]{:S(2)}, u32[]{:S(2)}) collective-permute-start(f32[16,4,64]{2,0,1:T(8,128)S(1)} %get-tuple-element.10), channel_id=1, source_target_pairs={{0,1},{1,2},{2,3},{3,4},{4,5},{5,6},{6,7},{7,8},{8,9},{9,10},{10,1... | collective-permute-start | bytes 49160 | tf_op jit(solution)/shard_map/ppermute | solution.py:23
  73.9 5.5 %collective-permute-start.11 = (f32[16,64]{1,0:T(8,128)S(1)}, f32[16,64]{1,0:T(8,128)S(1)}, u32[]{:S(2)}, u32[]{:S(2)}) collective-permute-start(f32[16,64]{1,0:T(8,128)S(1)} %add.143), channel_id=1, source_target_pairs={{0,4},{2,6},{4,0},{6,2},{1,5},{3,7},{5,1},{7,3},{8,12},{10,14},{12... | collective-permute-start | bytes 12296 | tf_op jit(solution)/shard_map/ppermute | solution.py:16
  77.5 20.6 %collective-permute-start.5 = (f32[2,16,64]{2,1,0:T(8,128)S(1)}, f32[2,16,64]{2,1,0:T(8,128)S(1)}, u32[]{:S(2)}, u32[]{:S(2)}) collective-permute-start(f32[2,16,64]{2,1,0:T(8,128)S(1)} %get-tuple-element.22), channel_id=1, source_target_pairs={{0,1},{1,2},{2,3},{3,4},{4,5},{5,6},{6,7},{7,8},{8,9},{9,10},{10,1... | collective-permute-start | bytes 24584 | tf_op jit(solution)/shard_map/ppermute | solution.py:23
  79.5 20.7 %collective-permute-start.8 = (f32[2,16,64]{2,1,0:T(8,128)S(1)}, f32[2,16,64]{2,1,0:T(8,128)S(1)}, u32[]{:S(2)}, u32[]{:S(2)}) collective-permute-start(f32[2,16,64]{2,1,0:T(8,128)S(1)} %get-tuple-element.23), channel_id=1, source_target_pairs={{1,0},{2,1},{3,2},{4,3},{5,4},{6,5},{7,6},{8,7},{9,8},{10,9},{11,1... | collective-permute-start | bytes 24584 | tf_op jit(solution)/shard_map/ppermute | solution.py:23
  98.2 12.9 %collective-permute-start.3 = (f32[16,4,64]{2,0,1:T(8,128)S(1)}, f32[16,4,64]{2,0,1:T(8,128)S(1)}, u32[]{:S(2)}, u32[]{:S(2)}) collective-permute-start(f32[16,4,64]{2,0,1:T(8,128)S(1)} %get-tuple-element.11), channel_id=1, source_target_pairs={{1,0},{2,1},{3,2},{4,3},{5,4},{6,5},{7,6},{8,7},{9,8},{10,9},{11,1... | collective-permute-start | bytes 49160 | tf_op jit(solution)/shard_map/ppermute | solution.py:23
  100.2 11.5 %collective-permute-start.6 = (f32[3,16,64]{2,1,0:T(8,128)S(1)}, f32[3,16,64]{2,1,0:T(8,128)S(1)}, u32[]{:S(2)}, u32[]{:S(2)}) collective-permute-start(f32[3,16,64]{2,1,0:T(8,128)S(1)} %get-tuple-element.20), channel_id=1, source_target_pairs={{0,1},{1,2},{2,3},{3,4},{4,5},{5,6},{6,7},{7,8},{8,9},{9,10},{10,1... | collective-permute-start | bytes 36872 | tf_op jit(solution)/shard_map/ppermute | solution.py:23
  102.6 9.1 %collective-permute-start.9 = (f32[3,16,64]{2,1,0:T(8,128)S(1)}, f32[3,16,64]{2,1,0:T(8,128)S(1)}, u32[]{:S(2)}, u32[]{:S(2)}) collective-permute-start(f32[3,16,64]{2,1,0:T(8,128)S(1)} %get-tuple-element.21), channel_id=1, source_target_pairs={{1,0},{2,1},{3,2},{4,3},{5,4},{6,5},{7,6},{8,7},{9,8},{10,9},{11,1... | collective-permute-start | bytes 36872 | tf_op jit(solution)/shard_map/ppermute | solution.py:23
  112.5 3.6 %copy-start.10 = (bf16[1,64,64]{2,1,0:T(8,128)(2,1)S(1)}, bf16[1,64,64]{2,1,0:T(8,128)(2,1)}, u32[]{:S(2)}) copy-start(bf16[1,64,64]{2,1,0:T(8,128)(2,1)} %param.24) | copy-start | bytes 24580
  114.3 55.3 %copy-start.3 = (bf16[16,16,256]{2,0,1:T(8,128)(2,1)}, bf16[16,16,256]{2,0,1:T(8,128)(2,1)S(1)}, u32[]{:S(2)}) copy-start(bf16[16,16,256]{2,0,1:T(8,128)(2,1)S(1)} %get-tuple-element.24) | copy-start | bytes 393220
  116.9 68.1 %collective-permute-start.19 = (f32[1,16,64]{2,1,0:T(8,128)}, f32[1,16,64]{2,1,0:T(8,128)}, u32[]{:S(2)}, u32[]{:S(2)}) collective-permute-start(f32[1,16,64]{2,1,0:T(8,128)} %bitcast.45), channel_id=1, source_target_pairs={{1,0},{2,1},{3,2},{4,3},{5,4},{6,5},{7,6},{8,7},{9,8},{10,9},{11,1... | collective-permute-start | bytes 12296 | tf_op jit(solution)/shard_map/ppermute | solution.py:23
  118.9 68.1 %collective-permute-start.16 = (f32[1,16,64]{2,1,0:T(8,128)}, f32[1,16,64]{2,1,0:T(8,128)}, u32[]{:S(2)}, u32[]{:S(2)}) collective-permute-start(f32[1,16,64]{2,1,0:T(8,128)} %bitcast.45), channel_id=1, source_target_pairs={{0,1},{1,2},{2,3},{3,4},{4,5},{5,6},{6,7},{7,8},{8,9},{9,10},{10,1... | collective-permute-start | bytes 12296 | tf_op jit(solution)/shard_map/ppermute | solution.py:23
  159.8 55.9 %collective-permute-start.12 = (bf16[16,2,256]{2,0,1:T(8,128)(2,1)}, bf16[16,2,256]{2,0,1:T(8,128)(2,1)}, u32[]{:S(2)}, u32[]{:S(2)}) collective-permute-start(bf16[16,2,256]{2,0,1:T(8,128)(2,1)} %get-tuple-element.8), channel_id=1, source_target_pairs={{0,1},{1,2},{2,3},{3,4},{4,5},{5,6},{6,7},{7,8},{8,9},{9,10},{10,1... | collective-permute-start | bytes 49160 | tf_op jit(solution)/shard_map/ppermute | solution.py:23
  161.7 58.3 %collective-permute-start.13 = (bf16[16,2,256]{2,0,1:T(8,128)(2,1)}, bf16[16,2,256]{2,0,1:T(8,128)(2,1)}, u32[]{:S(2)}, u32[]{:S(2)}) collective-permute-start(bf16[16,2,256]{2,0,1:T(8,128)(2,1)} %get-tuple-element.9), channel_id=1, source_target_pairs={{1,0},{2,1},{3,2},{4,3},{5,4},{6,5},{7,6},{8,7},{9,8},{10,9},{11,1... | collective-permute-start | bytes 49160 | tf_op jit(solution)/shard_map/ppermute | solution.py:23
  166.3 16.1 %collective-permute-start.22 = (f32[16,64]{1,0:T(8,128)}, f32[16,64]{1,0:T(8,128)}, u32[]{:S(2)}, u32[]{:S(2)}) collective-permute-start(f32[16,64]{1,0:T(8,128)} %fusion.14), channel_id=1, source_target_pairs={{0,2},{2,0},{4,6},{6,4},{1,3},{3,1},{5,7},{7,5},{8,10},{10,8},{12,... | collective-permute-start | bytes 12296 | tf_op jit(solution)/shard_map/ppermute | solution.py:16
  182.3 43.1 %collective-permute-start.14 = (f32[16,4,64]{2,0,1:T(8,128)}, f32[16,4,64]{2,0,1:T(8,128)S(1)}, u32[]{:S(2)}, u32[]{:S(2)}) collective-permute-start(f32[16,4,64]{2,0,1:T(8,128)} %get-tuple-element.6), channel_id=1, source_target_pairs={{0,1},{1,2},{2,3},{3,4},{4,5},{5,6},{6,7},{7,8},{8,9},{9,10},{10,1... | collective-permute-start | bytes 49160 | tf_op jit(solution)/shard_map/ppermute | solution.py:23
  185.0 5.3 %collective-permute-start.23 = (f32[16,64]{1,0:T(8,128)S(1)}, f32[16,64]{1,0:T(8,128)S(1)}, u32[]{:S(2)}, u32[]{:S(2)}) collective-permute-start(f32[16,64]{1,0:T(8,128)S(1)} %add.151), channel_id=1, source_target_pairs={{0,4},{2,6},{4,0},{6,2},{1,5},{3,7},{5,1},{7,3},{8,12},{10,14},{12... | collective-permute-start | bytes 12296 | tf_op jit(solution)/shard_map/ppermute | solution.py:16
  187.7 23.0 %collective-permute-start.17 = (f32[2,16,64]{2,1,0:T(8,128)S(1)}, f32[2,16,64]{2,1,0:T(8,128)S(1)}, u32[]{:S(2)}, u32[]{:S(2)}) collective-permute-start(f32[2,16,64]{2,1,0:T(8,128)S(1)} %get-tuple-element.18), channel_id=1, source_target_pairs={{0,1},{1,2},{2,3},{3,4},{4,5},{5,6},{6,7},{7,8},{8,9},{9,10},{10,1... | collective-permute-start | bytes 24584 | tf_op jit(solution)/shard_map/ppermute | solution.py:23
  190.3 22.3 %collective-permute-start.20 = (f32[2,16,64]{2,1,0:T(8,128)S(1)}, f32[2,16,64]{2,1,0:T(8,128)S(1)}, u32[]{:S(2)}, u32[]{:S(2)}) collective-permute-start(f32[2,16,64]{2,1,0:T(8,128)S(1)} %get-tuple-element.19), channel_id=1, source_target_pairs={{1,0},{2,1},{3,2},{4,3},{5,4},{6,5},{7,6},{8,7},{9,8},{10,9},{11,1... | collective-permute-start | bytes 24584 | tf_op jit(solution)/shard_map/ppermute | solution.py:23
  210.7 14.8 %collective-permute-start.15 = (f32[16,4,64]{2,0,1:T(8,128)}, f32[16,4,64]{2,0,1:T(8,128)S(1)}, u32[]{:S(2)}, u32[]{:S(2)}) collective-permute-start(f32[16,4,64]{2,0,1:T(8,128)} %get-tuple-element.7), channel_id=1, source_target_pairs={{1,0},{2,1},{3,2},{4,3},{5,4},{6,5},{7,6},{8,7},{9,8},{10,9},{11,1... | collective-permute-start | bytes 49160 | tf_op jit(solution)/shard_map/ppermute | solution.py:23
  213.3 12.8 %collective-permute-start.18 = (f32[3,16,64]{2,1,0:T(8,128)S(1)}, f32[3,16,64]{2,1,0:T(8,128)S(1)}, u32[]{:S(2)}, u32[]{:S(2)}) collective-permute-start(f32[3,16,64]{2,1,0:T(8,128)S(1)} %get-tuple-element.16), channel_id=1, source_target_pairs={{0,1},{1,2},{2,3},{3,4},{4,5},{5,6},{6,7},{7,8},{8,9},{9,10},{10,1... | collective-permute-start | bytes 36872 | tf_op jit(solution)/shard_map/ppermute | solution.py:23
  215.7 10.4 %collective-permute-start.21 = (f32[3,16,64]{2,1,0:T(8,128)S(1)}, f32[3,16,64]{2,1,0:T(8,128)S(1)}, u32[]{:S(2)}, u32[]{:S(2)}) collective-permute-start(f32[3,16,64]{2,1,0:T(8,128)S(1)} %get-tuple-element.17), channel_id=1, source_target_pairs={{1,0},{2,1},{3,2},{4,3},{5,4},{6,5},{7,6},{8,7},{9,8},{10,9},{11,1... | collective-permute-start | bytes 36872 | tf_op jit(solution)/shard_map/ppermute | solution.py:23
  221.7 3.8 %copy-start.12 = (s32[1024]{0:T(1024)S(1)}, s32[1024]{0:T(1024)}, u32[]{:S(2)}) copy-start(s32[1024]{0:T(1024)} %copy-done.11) | copy-start | bytes 12292
  221.7 5.2 %copy-start.7 = (bf16[1,64,192]{1,2,0:T(8,128)(2,1)S(1)}, bf16[1,64,192]{1,2,0:T(8,128)(2,1)}, u32[]{:S(2)}) copy-start(bf16[1,64,192]{1,2,0:T(8,128)(2,1)} %copy-done.6) | copy-start | bytes 73732
  221.7 5.3 %copy-start.2 = (bf16[16,64,64]{2,1,0:T(8,128)(2,1)S(1)}, bf16[16,64,64]{2,1,0:T(8,128)(2,1)}, u32[]{:S(2)}) copy-start(bf16[16,64,64]{2,1,0:T(8,128)(2,1)} %param.21) | copy-start | bytes 393220
